TPU v7x, 32 devices: a whole 2x2x4 slice. The times are simulated.
32 devices in a mesh: ga: 2 (over x), row: 8 (over z, y), col: 2 (over core).
Axes of the slice: x: 2, y: 2, z: 4, core: 2. Of those that a mesh axis runs over, the one named last changes fastest.
Arguments:
- pair: bfloat16 [256, 128, 128], P(('ga', 'row', 'col')), parts along dimension 0, may hold values from -480 to 480
- residue_mask: int32 [256], P('ga'), parts along dimension 0, may hold values from 0 to 1, as said below
- targets: int32 [256, 128], P(('ga', 'row', 'col')), parts along dimension 0, may hold values from 0 to 63
- ln_gain: float32 [2, 128], replicated, may hold values from 0.25 to 1.75
- ln_shift: float32 [2, 128], replicated, may hold values from -3 to 3
- w_in: bfloat16 [5, 128, 128], P(None, None, 'col'), may hold values from -0.5 to 0.5
- b_in: float32 [5, 128], replicated, may hold values from -3 to 3
- w_out: bfloat16 [128, 128], P('col'), may hold values from -0.5 to 0.5
- b_out: float32 [128], replicated, may hold values from -3 to 3
- head_weight: bfloat16 [128, 64], replicated, may hold values from -0.5 to 0.5
- head_bias: float32 [64], replicated, may hold values from -4 to 4
Outputs:
- update: bfloat16 [256, 128, 128], P(('ga', 'row', 'col')), parts along dimension 0
- pair_loss: float32 [256, 128], P(('ga', 'row', 'col')), parts along dimension 0
There are 2 independent parts, one for each index of `ga`. A program takes and returns all parts, laid end to end along the dimension named above; an argument that names none is the same for every part. Nothing has to cross between parts.
Inputs may be any that keep to these rules, and one draw needn't show every extreme that they name: `residue_mask`: each part's entries are 1 for residues 0 to some length - 1 and 0 after it; the length is at least 64 and at most 128.
All inputs are finite; a program needn't handle non-finite values.
Results may differ from a plain program's by a relative error of at most 0.0055.
Values may be sent and summed in bfloat16 or wider, within the bound.
A program may use at most 64 MiB of HBM per device.

v0:
```python
import functools

import jax
import jax.numpy as jnp
from jax import lax
from jax.experimental import pallas as pl
from jax.experimental.pallas import tpu as pltpu
from jax.sharding import PartitionSpec as P

SUPER = 2
CHUNKS = 2
EIGHTHS = 4
F32, BF16 = jnp.float32, jnp.bfloat16
NT = (((1,), (1,)), ((), ()))
TN = (((0,), (0,)), ((), ()))


def dot(lhs, rhs, dims=(((1,), (0,)), ((), ()))):
    return lax.dot_general(lhs, rhs, dims, preferred_element_type=F32)


def kernel(
    rows_n, cols_n, sup, chunks,
    *refs,
):
    sources, (update, loss) = refs[:11], refs[11:13]
    held, rest = refs[13:24], refs[24:]
    (pair, mask, targets, ln_gain, ln_shift, w_in, b_in, w_out, b_out, head_w, head_b) = held
    (
    wt, wo, small, normed, side_f, right_b, left_b, left_in, right_in, prod, outer, outer_f, gate,
        new_pair, logit_b, logit_in, logit_f, own_t,
        w_send, w_recv, l_send, l_recv, r_send, r_recv, o_send, o_recv, m_send, m_recv,
        in_sem,
    ) = rest
    groups = rows_n * cols_n
    count, length, width = pair.shape
    bins = head_w.shape[0]
    per = groups // sup
    share = width // per
    first = max(share * EIGHTHS // 8, 1)
    edges = [0, first, share] if chunks > 1 else [0, share]
    half = w_in.shape[1]
    lanes = 128
    spans = length // lanes
    packed = 128 // bins
    quads = count // packed
    col = lax.axis_index("col")
    me = lax.axis_index("row") * cols_n + col
    block, slot = lax.div(me, per), lax.rem(me, per)

    def where(peer):
        return {"row": lax.div(peer, cols_n), "col": lax.rem(peer, cols_n)}

    def remote(src, dst, send, recv, peer):
        return pltpu.make_async_remote_copy(
            src_ref=src, dst_ref=dst, send_sem=send, recv_sem=recv,
            device_id=where(peer), device_id_type=pl.DeviceIdType.MESH,
        )

    def each(n, body):
        lax.fori_loop(0, n, lambda i, c: (body(i), c)[1], 0, unroll=True)

    loads = [pltpu.make_async_copy(sources[n], held[n], in_sem.at[n]) for n in range(11)]
    for load in loads:
        load.start()
    barrier = pltpu.get_barrier_semaphore()

    def greet(d):
        pl.semaphore_signal(
            barrier, inc=1, device_id=where(lax.rem(me + 1 + d, groups)),
            device_id_type=pl.DeviceIdType.MESH,
        )

    each(groups - 1, greet)

    def drain(ref, sem):
        pltpu.make_async_copy(ref, ref, sem).wait()


    for load in loads:
        load.wait()
    mine = pl.ds(pl.multiple_of(col * half, half), half)
    wt[:, mine, :] = w_in[...]
    wo[mine, :] = w_out[...]

    def norm_rows(i):
        values = pair[i].astype(F32)
        centred = values - jnp.mean(values, axis=-1, keepdims=True)
        spread = jnp.mean(centred * centred, axis=-1, keepdims=True)
        scaled = centred * lax.rsqrt(spread + 0.1) * ln_gain[0:1, :] + ln_shift[0:1, :]
        normed[i] = scaled.astype(BF16)

    each(count, norm_rows)

    row_mask = mask[...].astype(F32)
    lane = lax.broadcasted_iota(jnp.int32, (count, length), 1)
    sub = lax.broadcasted_iota(jnp.int32, (count, length), 0)
    own_mask = jnp.sum(jnp.where(lane == me * count + sub, row_mask, 0.0), axis=1, keepdims=True)
    pair_mask = own_mask * row_mask

    small[...] = jnp.concatenate(
        [b_in[...], ln_gain[1:2, :], ln_shift[1:2, :], jnp.zeros((1, width), F32)], axis=0
    ).T

    pl.semaphore_wait(barrier, groups - 1)

    def weight_copies(peer_col):
        peer = me - col + peer_col
        return (
            remote(wt.at[:, mine, :], wt.at[:, mine, :], w_send.at[0, peer_col], w_recv.at[0, col], peer),
            remote(wo.at[mine, :], wo.at[mine, :], w_send.at[1, peer_col], w_recv.at[1, col], peer),
        )

    for d in range(1, cols_n):
        for copy in weight_copies(lax.rem(col + d, cols_n)):
            copy.start()

    def wait_weights(which):
        for d in range(1, cols_n):
            peer_col = lax.rem(col + d, cols_n)
            theirs = pl.ds(pl.multiple_of(peer_col * half, half), half)
            ref = (wt.at[:, theirs, :], wo.at[theirs, :])[which]
            mine_ref = (wt.at[:, mine, :], wo.at[mine, :])[which]
            peer = me - col + peer_col
            remote(ref, ref, w_send.at[which, peer_col], w_recv.at[which, peer_col], peer).wait_recv()
            remote(mine_ref, mine_ref, w_send.at[which, peer_col], w_recv.at[which, peer_col], peer).wait_send()

    def make_side(first, out, span_w):
        start = pl.multiple_of(span_w * half, half)
        rows = pl.ds(start, half)
        weights = wt[first:first + 2, rows, :].reshape(2 * half, width)
        value_b, gate_b = small[rows, first:first + 1], small[rows, first + 1:first + 2]

        for i in range(count):
            both = dot(weights, normed[i], NT)
            value = jax.nn.sigmoid(both[half:] + gate_b) * (both[:half] + value_b)
            for b in range(spans):
                side_f[b, pl.ds(i, half, stride=count), :] = value[:, b * lanes:(b + 1) * lanes]
        for b in range(spans):
            span = slice(b * lanes, (b + 1) * lanes)
            masked = side_f[b].reshape(half, count, lanes) * pair_mask[:, span][None]
            out[rows, :, span] = masked.astype(BF16)

    def channels(owner, ch):
        return pl.ds(owner * share + edges[ch], edges[ch + 1] - edges[ch])

    def left_copy(dest, ch):
        return remote(
            left_b.at[channels(dest, ch)],
            left_in.at[slot, pl.ds(edges[ch], edges[ch + 1] - edges[ch])],
            l_send.at[ch], l_recv.at[ch], block * per + dest,
        )

    def right_copy(dest, ch):
        return remote(
            right_b.at[channels(lax.rem(dest, per), ch)],
            right_in.at[me, pl.ds(edges[ch], edges[ch + 1] - edges[ch])],
            r_send.at[ch], r_recv.at[ch], dest,
        )

    def right_local(ch):
        return pltpu.make_async_copy(
            right_b.at[channels(slot, ch)],
            right_in.at[me, pl.ds(edges[ch], edges[ch + 1] - edges[ch])],
            r_recv.at[ch],
        )

    def left_local(ch):
        return pltpu.make_async_copy(
            left_b.at[channels(slot, ch)],
            left_in.at[slot, pl.ds(edges[ch], edges[ch + 1] - edges[ch])],
            l_recv.at[ch],
        )

    quota = per // cols_n

    def send_right(ch, span_w):
        def one(d):
            owner = span_w * quota + lax.rem(slot + d, quota)
            dest = lax.rem(block * per + owner + lax.div(d, quota) * per, groups)

            @pl.when(dest != me)
            def _():
                right_copy(dest, ch).start()

        each(sup * quota, one)

    def send_left(ch, span_w):
        def one(d):
            owner = span_w * quota + lax.rem(slot + d, quota)

            @pl.when(owner != slot)
            def _():
                left_copy(owner, ch).start()

        each(quota, one)

    for turn in range(cols_n):
        if turn == 1:
            wait_weights(0)
        span_w = lax.rem(col + turn, cols_n)
        make_side(2, right_b, span_w)
        send_right(0, span_w)
    right_local(0).start()
    for turn in range(cols_n):
        span_w = lax.rem(col + turn, cols_n)
        make_side(0, left_b, span_w)
        send_left(0, span_w)
    left_local(0).start()
    for ch in range(1, chunks):
        for turn in range(cols_n):
            send_right(ch, lax.rem(col + turn, cols_n))
        right_local(ch).start()
        for turn in range(cols_n):
            send_left(ch, lax.rem(col + turn, cols_n))
        left_local(ch).start()

    def make_gate(i):
        gate[i] = jax.nn.sigmoid(dot(normed[i], wt[4], NT) + b_in[4:5, :])

    each(count, make_gate)
    wait_weights(1)

    def outer_copy(dest, ch):
        return remote(
            prod.at[dest, pl.ds(edges[ch], edges[ch + 1] - edges[ch])],
            outer.at[channels(slot, ch)],
            o_send.at[ch], o_recv.at[ch], block * per + dest,
        )

    def outer_local(ch):
        return pltpu.make_async_copy(
            prod.at[slot, pl.ds(edges[ch], edges[ch + 1] - edges[ch])],
            outer.at[channels(slot, ch)],
            o_recv.at[ch],
        )

    for ch in range(chunks):
        now = pl.ds(edges[ch], edges[ch + 1] - edges[ch])
        drain(left_in.at[:, now], l_recv.at[ch])
        drain(right_in.at[:, now], r_recv.at[ch])
        for c in range(edges[ch], edges[ch + 1]):
            lhs = left_in[:, c].reshape(per * count, length)
            rhs = right_in[:, c].reshape(length, length)
            prod[:, c] = dot(lhs, rhs, NT).astype(BF16).reshape(per, count, length)
        each(per - 1, lambda d: outer_copy(lax.rem(slot + 1 + d, per), ch).start())
        outer_local(ch).start()

    for ch in range(chunks):
        drain(prod.at[:, pl.ds(edges[ch], edges[ch + 1] - edges[ch])], o_recv.at[ch])

    head_t = head_w[...]
    blank = jnp.zeros((bins, width), BF16)
    spread_w = [
        jnp.concatenate([head_t if h == p else blank for h in range(packed)], axis=0)
        for p in range(packed)
    ]
    bias_row = jnp.concatenate([head_b[...]] * packed, axis=1)

    gain_col, shift_col = small[:, 5:6], small[:, 6:7]
    for b in range(spans):
        span = slice(b * lanes, (b + 1) * lanes)
        values = outer[:, :, span].astype(F32)
        average = jnp.sum(values, axis=0) * (1.0 / width)
        outer_f[b] = values.reshape(width * count, lanes)
        centred = values - average[None]
        inverse = lax.rsqrt(jnp.sum(centred * centred, axis=0) * (1.0 / width) + 1.0)
        for i in range(count):
            part_i = outer_f[b, pl.ds(i, width, stride=count), :]
            part_i = (part_i - average[i:i + 1, :]) * inverse[i:i + 1, :] * gain_col + shift_col
            mixed = dot(part_i.astype(BF16), wo[...], TN) + b_out[...]
            rounded = (gate[i, span, :] * mixed).astype(BF16)
            update[i, span, :] = rounded
            new_pair[i, span, :] = (pair[i, span, :].astype(F32) + rounded.astype(F32)).astype(BF16)
    for i in range(quads):
        total = bias_row
        for p in range(packed):
            total = total + dot(new_pair[p * quads + i], spread_w[p], NT)
        logit_b[:, i] = total.astype(BF16).reshape(groups, count, 128)

    def logit_copy(dest):
        return remote(
            logit_b.at[dest], logit_in.at[me],
            m_send.at[0], m_recv.at[0], dest,
        )

    logit_local = pltpu.make_async_copy(
        logit_b.at[me], logit_in.at[me], m_recv.at[0]
    )
    each(groups - 1, lambda d: logit_copy(lax.rem(me + 1 + d, groups)).start())
    logit_local.start()

    bias_col = jnp.concatenate([head_b[...], jnp.zeros((7, bins), F32)], axis=0).T[:, 0:1]
    for i in range(count):
        own_t[i] = dot(head_t, new_pair[i], NT) + bias_col
    at = lax.broadcasted_iota(jnp.int32, (length, length), 0)
    to = lax.broadcasted_iota(jnp.int32, (length, length), 1)
    fold = length // packed
    order = ((at % fold) // quads) * count + (at // fold) * quads + at % quads
    shuffle = jnp.where(order == to, 1.0, 0.0).astype(BF16)

    drain(logit_in, m_recv.at[0])
    logit_f[...] = logit_in[...].astype(F32).reshape(logit_f.shape)
    bin_id = lax.broadcasted_iota(jnp.int32, (bins, length), 0)
    for i in range(count):
        flipped = logit_f[pl.ds(i, groups * quads, stride=count), :].T
        flipped = jnp.concatenate([flipped[p * bins:(p + 1) * bins] for p in range(packed)], axis=1)
        symmetric = own_t[i] + dot(flipped.astype(BF16), shuffle)
        top = jnp.max(symmetric, axis=0, keepdims=True)
        total = top + jnp.log(jnp.sum(jnp.exp(symmetric - top), axis=0, keepdims=True))
        chosen = jnp.sum(jnp.where(bin_id == targets[i:i + 1, :], symmetric, 0.0), axis=0, keepdims=True)
        loss[i:i + 1, :] = pair_mask[i:i + 1, :] * (total - chosen)

    for ch in range(chunks):
        now = pl.ds(edges[ch], edges[ch + 1] - edges[ch])
        drain(left_in.at[pl.ds(0, per - 1), now], l_send.at[ch])
        drain(right_in.at[pl.ds(0, groups - 1), now], r_send.at[ch])
        drain(prod.at[pl.ds(0, per - 1), now], o_send.at[ch])
    drain(logit_in.at[pl.ds(0, groups - 1)], m_send.at[0])


def local(rows_n, cols_n, *args):
    pair, residue_mask, targets, ln_gain, ln_shift, w_in, b_in, w_out, b_out, head_w, head_b = args
    count, length, width = pair.shape
    bins = head_w.shape[1]
    groups = rows_n * cols_n
    sup = SUPER
    per = groups // sup
    share = width // per
    chunks = CHUNKS
    packed = 128 // bins
    quads = count // packed
    dma = pltpu.SemaphoreType.DMA
    vmem = pl.BlockSpec(memory_space=pltpu.VMEM)
    inputs = (
        pair, residue_mask.reshape(1, length), targets, ln_gain, ln_shift,
        jnp.swapaxes(w_in, 1, 2), b_in, w_out, b_out.reshape(1, width), head_w.T,
        head_b.reshape(1, bins),
    )
    return pl.pallas_call(
        functools.partial(kernel, rows_n, cols_n, sup, chunks),
        out_shape=(
            pltpu.VMEM(pair.shape, BF16),
            pltpu.VMEM((count, length), F32),
        ),
        in_specs=[pl.BlockSpec(memory_space=pl.ANY)] * 11,
        out_specs=(vmem, vmem),
        scratch_shapes=[pltpu.VMEM(x.shape, x.dtype) for x in inputs] + [
            pltpu.VMEM((5, width, width), BF16),
            pltpu.VMEM((width, width), BF16),
            pltpu.VMEM((width, 8), F32),
            pltpu.VMEM((count, length, width), BF16),
            pltpu.VMEM((length // 128, width // cols_n * count, 128), F32),
            pltpu.VMEM((width, count, length), BF16),
            pltpu.VMEM((width, count, length), BF16),
            pltpu.VMEM((per, share, count, length), BF16),
            pltpu.VMEM((groups, share, count, length), BF16),
            pltpu.VMEM((per, share, count, length), BF16),
            pltpu.VMEM((width, count, length), BF16),
            pltpu.VMEM((length // 128, width * count, 128), F32),
            pltpu.VMEM((count, length, width), F32),
            pltpu.VMEM((count, length, width), BF16),
            pltpu.VMEM((groups, quads, count, 128), BF16),
            pltpu.VMEM((groups, quads, count, 128), BF16),
            pltpu.VMEM((groups * quads * count, 128), F32),
            pltpu.VMEM((count, bins, length), F32),
            dma((2, cols_n)), dma((2, cols_n)),
            dma((chunks,)), dma((chunks,)), dma((chunks,)), dma((chunks,)), dma((chunks,)), dma((chunks,)),
            dma((1,)), dma((1,)),
            dma((11,)),
        ],
        compiler_params=pltpu.CompilerParams(
            collective_id=0, has_side_effects=True, vmem_limit_bytes=60 * 1024 * 1024
        ),
    )(*inputs)


def solution(mesh):
    placed = (
        P(("ga", "row", "col"), None, None),
        P("ga"),
        P(("ga", "row", "col"), None),
        P(),
        P(),
        P(None, None, "col"),
        P(),
        P("col", None),
        P(),
        P(),
        P(),
    )
    return jax.shard_map(
        functools.partial(local, mesh.shape["row"], mesh.shape["col"]),
        mesh=mesh,
        in_specs=placed,
        out_specs=(P(("ga", "row", "col"), None, None), P(("ga", "row", "col"), None)),
        check_vma=False,
    )
```

profile of v0, /device:TPU:0, one launch (start us, length us, event | category | flops | bytes accessed | tf_op | source)
XLA Modules:
  0.0 31.6 jit_solution(582090295916394782)
XLA Ops:
  0.6 29.6 %shard_map.122 = (bf16[8,128,128]{2,1,0:T(8,128)(2,1)S(1)}, f32[8,128]{1,0:T(8,128)S(1)}) custom-call(bf16[8,128,128]{2,1,0:T(8,128)(2,1)} %refs_0_.1, s32[1,128]{1,0:T(1,128)} %bitcast.7, s32[8,128]{1,0:T(8,128)} %refs_2_.1, f32[2,128]{1,0:T(2,128)} %refs_3_.1, f32[2,128]{1,0:T(2,128)} %refs_4_.1, bf16[5,64,128]{2,1,0:T(8,128)(2,1)} %bitcast.5, ...), custom_call_target="tpu_custom_call" | custom-call | tf_op jit(solution)/shard_map/pallas_call | solution.py:340
  30.3 0.7 %copy.15 = bf16[8,128,128]{2,1,0:T(8,128)(2,1)} copy(bf16[8,128,128]{2,1,0:T(8,128)(2,1)S(1)} %get-tuple-element.2) | data formatting | bytes 524288
  31.0 0.6 %copy.16 = f32[8,128]{1,0:T(8,128)} copy(f32[8,128]{1,0:T(8,128)S(1)} %get-tuple-element.3) | data formatting | bytes 8192
where the time goes:
time: 31.7 us; the launch traced here: 31.6 us
  Pallas kernels  29.6 us (93%)
  local copies, waits for them, and re-layouts  1.3 us (4%)
  between operations  0.64 us (2%)
    pallas_call x1, Pallas kernels, local(): pl.pallas_call(functools.partial(kernel, rows_n, cols_n, sup, chunks), ou...  29.6 us
    unnamed x2, local copies, waits for them, and re-layouts  1.3 us

commit v1 on v0

--- a/solution.py
+++ b/solution.py
@@ -8,8 +8,6 @@
 from jax.sharding import PartitionSpec as P
 
 SUPER = 2
-CHUNKS = 2
-EIGHTHS = 4
 F32, BF16 = jnp.float32, jnp.bfloat16
 NT = (((1,), (1,)), ((), ()))
 TN = (((0,), (0,)), ((), ()))
@@ -20,7 +18,7 @@
 
 
 def kernel(
-    rows_n, cols_n, sup, chunks,
+    rows_n, cols_n, sup,
     *refs,
 ):
     sources, (update, loss) = refs[:11], refs[11:13]
@@ -37,8 +35,7 @@
     bins = head_w.shape[0]
     per = groups // sup
     share = width // per
-    first = max(share * EIGHTHS // 8, 1)
-    edges = [0, first, share] if chunks > 1 else [0, share]
+    part = share // cols_n
     half = w_in.shape[1]
     lanes = 128
     spans = length // lanes
@@ -47,6 +44,8 @@
     col = lax.axis_index("col")
     me = lax.axis_index("row") * cols_n + col
     block, slot = lax.div(me, per), lax.rem(me, per)
+    plane = per // 2
+    inner = (lax.div(slot, plane) + block) % 2 == 1
 
     def where(peer):
         return {"row": lax.div(peer, cols_n), "col": lax.rem(peer, cols_n)}
@@ -102,18 +101,12 @@
         [b_in[...], ln_gain[1:2, :], ln_shift[1:2, :], jnp.zeros((1, width), F32)], axis=0
     ).T
 
-    pl.semaphore_wait(barrier, groups - 1)
-
     def weight_copies(peer_col):
         peer = me - col + peer_col
         return (
             remote(wt.at[:, mine, :], wt.at[:, mine, :], w_send.at[0, peer_col], w_recv.at[0, col], peer),
             remote(wo.at[mine, :], wo.at[mine, :], w_send.at[1, peer_col], w_recv.at[1, col], peer),
         )
-
-    for d in range(1, cols_n):
-        for copy in weight_copies(lax.rem(col + d, cols_n)):
-            copy.start()
 
     def wait_weights(which):
         for d in range(1, cols_n):
@@ -141,79 +134,60 @@
             masked = side_f[b].reshape(half, count, lanes) * pair_mask[:, span][None]
             out[rows, :, span] = masked.astype(BF16)
 
-    def channels(owner, ch):
-        return pl.ds(owner * share + edges[ch], edges[ch + 1] - edges[ch])
-
-    def left_copy(dest, ch):
+    def channels(owner, h):
+        return pl.ds(h * half + owner * part, part)
+
+    def places(h):
+        return pl.ds(h * part, part)
+
+    def left_copy(dest, h):
         return remote(
-            left_b.at[channels(dest, ch)],
-            left_in.at[slot, pl.ds(edges[ch], edges[ch + 1] - edges[ch])],
-            l_send.at[ch], l_recv.at[ch], block * per + dest,
-        )
-
-    def right_copy(dest, ch):
+            left_b.at[channels(dest, h)], left_in.at[slot, places(h)],
+            l_send.at[h], l_recv.at[h], block * per + dest,
+        )
+
+    def right_copy(dest, h):
         return remote(
-            right_b.at[channels(lax.rem(dest, per), ch)],
-            right_in.at[me, pl.ds(edges[ch], edges[ch + 1] - edges[ch])],
-            r_send.at[ch], r_recv.at[ch], dest,
-        )
-
-    def right_local(ch):
-        return pltpu.make_async_copy(
-            right_b.at[channels(slot, ch)],
-            right_in.at[me, pl.ds(edges[ch], edges[ch + 1] - edges[ch])],
-            r_recv.at[ch],
-        )
-
-    def left_local(ch):
-        return pltpu.make_async_copy(
-            left_b.at[channels(slot, ch)],
-            left_in.at[slot, pl.ds(edges[ch], edges[ch + 1] - edges[ch])],
-            l_recv.at[ch],
-        )
-
-    quota = per // cols_n
-
-    def send_right(ch, span_w):
+            right_b.at[channels(lax.rem(dest, per), h)], right_in.at[me, places(h)],
+            r_send.at[h], r_recv.at[h], dest,
+        )
+
+    def send_block(h):
         def one(d):
-            owner = span_w * quota + lax.rem(slot + d, quota)
-            dest = lax.rem(block * per + owner + lax.div(d, quota) * per, groups)
-
-            @pl.when(dest != me)
-            def _():
-                right_copy(dest, ch).start()
-
-        each(sup * quota, one)
-
-    def send_left(ch, span_w):
+            owner = lax.rem(slot + 1 + d, per)
+            right_copy(block * per + owner, h).start()
+            left_copy(owner, h).start()
+
+        each(per - 1, one)
+
+    def send_across(h):
         def one(d):
-            owner = span_w * quota + lax.rem(slot + d, quota)
-
-            @pl.when(owner != slot)
-            def _():
-                left_copy(owner, ch).start()
-
-        each(quota, one)
-
+            near = lax.rem(lax.div(d, plane) + block, 2)
+            owner = near * plane + lax.rem(slot + d, plane)
+            right_copy((1 - block) * per + owner, h).start()
+
+        each(per, one)
+
+    def keep(h):
+        pltpu.make_async_copy(right_b.at[channels(slot, h)], right_in.at[me, places(h)], r_recv.at[h]).start()
+        pltpu.make_async_copy(left_b.at[channels(slot, h)], left_in.at[slot, places(h)], l_recv.at[h]).start()
+
+    make_side(2, right_b, col)
+    pl.semaphore_wait(barrier, groups - 1)
+    for d in range(1, cols_n):
+        for copy in weight_copies(lax.rem(col + d, cols_n)):
+            copy.start()
     for turn in range(cols_n):
-        if turn == 1:
-            wait_weights(0)
-        span_w = lax.rem(col + turn, cols_n)
-        make_side(2, right_b, span_w)
-        send_right(0, span_w)
-    right_local(0).start()
-    for turn in range(cols_n):
-        span_w = lax.rem(col + turn, cols_n)
-        make_side(0, left_b, span_w)
-        send_left(0, span_w)
-    left_local(0).start()
-    for ch in range(1, chunks):
-        for turn in range(cols_n):
-            send_right(ch, lax.rem(col + turn, cols_n))
-        right_local(ch).start()
-        for turn in range(cols_n):
-            send_left(ch, lax.rem(col + turn, cols_n))
-        left_local(ch).start()
+        h = lax.rem(col + turn, cols_n)
+        if turn:
+            if turn == 1:
+                wait_weights(0)
+            make_side(2, right_b, h)
+        send_across(h)
+        make_side(0, left_b, h)
+        send_block(h)
+        keep(h)
+
 
     def make_gate(i):
         gate[i] = jax.nn.sigmoid(dot(normed[i], wt[4], NT) + b_in[4:5, :])
@@ -221,33 +195,24 @@
     each(count, make_gate)
     wait_weights(1)
 
-    def outer_copy(dest, ch):
+    def outer_copy(dest, h):
         return remote(
-            prod.at[dest, pl.ds(edges[ch], edges[ch + 1] - edges[ch])],
-            outer.at[channels(slot, ch)],
-            o_send.at[ch], o_recv.at[ch], block * per + dest,
-        )
-
-    def outer_local(ch):
-        return pltpu.make_async_copy(
-            prod.at[slot, pl.ds(edges[ch], edges[ch + 1] - edges[ch])],
-            outer.at[channels(slot, ch)],
-            o_recv.at[ch],
-        )
-
-    for ch in range(chunks):
-        now = pl.ds(edges[ch], edges[ch + 1] - edges[ch])
-        drain(left_in.at[:, now], l_recv.at[ch])
-        drain(right_in.at[:, now], r_recv.at[ch])
-        for c in range(edges[ch], edges[ch + 1]):
+            prod.at[dest, places(h)], outer.at[channels(slot, h)],
+            o_send.at[h], o_recv.at[h], block * per + dest,
+        )
+
+    for h in range(cols_n):
+        drain(left_in.at[:, places(h)], l_recv.at[h])
+        drain(right_in.at[:, places(h)], r_recv.at[h])
+        for c in range(h * part, (h + 1) * part):
             lhs = left_in[:, c].reshape(per * count, length)
             rhs = right_in[:, c].reshape(length, length)
             prod[:, c] = dot(lhs, rhs, NT).astype(BF16).reshape(per, count, length)
-        each(per - 1, lambda d: outer_copy(lax.rem(slot + 1 + d, per), ch).start())
-        outer_local(ch).start()
-
-    for ch in range(chunks):
-        drain(prod.at[:, pl.ds(edges[ch], edges[ch + 1] - edges[ch])], o_recv.at[ch])
+        each(per - 1, lambda d: outer_copy(lax.rem(slot + 1 + d, per), h).start())
+        pltpu.make_async_copy(prod.at[slot, places(h)], outer.at[channels(slot, h)], o_recv.at[h]).start()
+
+    for h in range(cols_n):
+        drain(prod.at[:, places(h)], o_recv.at[h])
 
     head_t = head_w[...]
     blank = jnp.zeros((bins, width), BF16)
@@ -311,12 +276,20 @@
         chosen = jnp.sum(jnp.where(bin_id == targets[i:i + 1, :], symmetric, 0.0), axis=0, keepdims=True)
         loss[i:i + 1, :] = pair_mask[i:i + 1, :] * (total - chosen)
 
-    for ch in range(chunks):
-        now = pl.ds(edges[ch], edges[ch + 1] - edges[ch])
-        drain(left_in.at[pl.ds(0, per - 1), now], l_send.at[ch])
-        drain(right_in.at[pl.ds(0, groups - 1), now], r_send.at[ch])
-        drain(prod.at[pl.ds(0, per - 1), now], o_send.at[ch])
+    for h in range(cols_n):
+        drain(left_in.at[pl.ds(0, per - 1), places(h)], l_send.at[h])
+        drain(right_in.at[pl.ds(0, groups - 1), places(h)], r_send.at[h])
+        drain(prod.at[pl.ds(0, per - 1), places(h)], o_send.at[h])
     drain(logit_in.at[pl.ds(0, groups - 1)], m_send.at[0])
+
+
+def finish(update, loss, update_out, loss_out, sem):
+    first = pltpu.make_async_copy(update, update_out, sem.at[0])
+    second = pltpu.make_async_copy(loss, loss_out, sem.at[1])
+    first.start()
+    second.start()
+    first.wait()
+    second.wait()
 
 
 def local(rows_n, cols_n, *args):
@@ -327,7 +300,7 @@
     sup = SUPER
     per = groups // sup
     share = width // per
-    chunks = CHUNKS
+    chunks = cols_n
     packed = 128 // bins
     quads = count // packed
     dma = pltpu.SemaphoreType.DMA
@@ -337,8 +310,8 @@
         jnp.swapaxes(w_in, 1, 2), b_in, w_out, b_out.reshape(1, width), head_w.T,
         head_b.reshape(1, bins),
     )
-    return pl.pallas_call(
-        functools.partial(kernel, rows_n, cols_n, sup, chunks),
+    update, loss = pl.pallas_call(
+        functools.partial(kernel, rows_n, cols_n, sup),
         out_shape=(
             pltpu.VMEM(pair.shape, BF16),
             pltpu.VMEM((count, length), F32),
@@ -373,6 +346,16 @@
             collective_id=0, has_side_effects=True, vmem_limit_bytes=60 * 1024 * 1024
         ),
     )(*inputs)
+    anywhere = pl.BlockSpec(memory_space=pl.ANY)
+    return pl.pallas_call(
+        finish,
+        out_shape=(
+            jax.ShapeDtypeStruct(update.shape, update.dtype), jax.ShapeDtypeStruct(loss.shape, loss.dtype),
+        ),
+        in_specs=[pl.BlockSpec(memory_space=pltpu.VMEM)] * 2, compiler_params=pltpu.CompilerParams(vmem_limit_bytes=1024*1024),
+        out_specs=(anywhere, anywhere),
+        scratch_shapes=[dma((2,))],
+    )(update, loss)
 
 
 def solution(mesh):

time: 31.7 us -> 30.8 us (0.972)
  local copies, waits for them, and re-layouts: 1.3 us -> 0 us
  Pallas kernels: 29.6 us -> 30.1 us
    unnamed x2 -> x0, local copies, waits for them, and re-layouts: 1.3 us -> none
    pallas_call x1 -> x2, Pallas kernels: 29.6 us -> 30.1 us  [the longest x1 29.3 us: local(): pl.pallas_call(functools.partial(kernel, rows_n, cols_n, sup), out_shape=...]
where the time goes in v1:
time: 30.8 us; the launch traced here: 30.7 us
  Pallas kernels  30.1 us (98%)
  between operations  0.64 us (2%)
    pallas_call x1, Pallas kernels, local(): pl.pallas_call(functools.partial(kernel, rows_n, cols_n, sup), out_shape=...  29.3 us
    pallas_call x1, Pallas kernels, local(): pl.pallas_call(finish, out_shape=(jax.ShapeDtypeStruct(update.shape, upda...  0.72 us

profile of v1, /device:TPU:0, one launch (start us, length us, event | category | flops | bytes accessed | tf_op | source)
XLA Modules:
  0.0 30.7 jit_solution(9372242197275463267)
XLA Ops:
  0.6 29.3 %shard_map.122 = (bf16[8,128,128]{2,1,0:T(8,128)(2,1)S(1)}, f32[8,128]{1,0:T(8,128)S(1)}) custom-call(bf16[8,128,128]{2,1,0:T(8,128)(2,1)} %refs_0_.1, s32[1,128]{1,0:T(1,128)} %bitcast.7, s32[8,128]{1,0:T(8,128)} %refs_2_.1, f32[2,128]{1,0:T(2,128)} %refs_3_.1, f32[2,128]{1,0:T(2,128)} %refs_4_.1, bf16[5,64,128]{2,1,0:T(8,128)(2,1)} %bitcast.5, ...), custom_call_target="tpu_custom_call" | custom-call | tf_op jit(solution)/shard_map/pallas_call | solution.py:313
  30.0 0.7 %shard_map.123 = (bf16[8,128,128]{2,1,0:T(8,128)(2,1)}, f32[8,128]{1,0:T(8,128)}) custom-call(bf16[8,128,128]{2,1,0:T(8,128)(2,1)S(1)} %get-tuple-element.4.update, f32[8,128]{1,0:T(8,128)S(1)} %get-tuple-element.5.loss), custom_call_target="tpu_custom_call" | custom-call | tf_op jit(solution)/shard_map/pallas_call | solution.py:350

commit v2 on v1

--- a/solution.py
+++ b/solution.py
@@ -8,6 +8,7 @@
 from jax.sharding import PartitionSpec as P
 
 SUPER = 2
+CUT = 5
 F32, BF16 = jnp.float32, jnp.bfloat16
 NT = (((1,), (1,)), ((), ()))
 TN = (((0,), (0,)), ((), ()))
@@ -18,7 +19,7 @@
 
 
 def kernel(
-    rows_n, cols_n, sup,
+    rows_n, cols_n, sup, chunks,
     *refs,
 ):
     sources, (update, loss) = refs[:11], refs[11:13]
@@ -36,6 +37,8 @@
     per = groups // sup
     share = width // per
     part = share // cols_n
+    cut = max(part * CUT // 8, 1)
+    edges = [0, cut, part]
     half = w_in.shape[1]
     lanes = 128
     spans = length // lanes
@@ -45,7 +48,6 @@
     me = lax.axis_index("row") * cols_n + col
     block, slot = lax.div(me, per), lax.rem(me, per)
     plane = per // 2
-    inner = (lax.div(slot, plane) + block) % 2 == 1
 
     def where(peer):
         return {"row": lax.div(peer, cols_n), "col": lax.rem(peer, cols_n)}
@@ -132,45 +134,49 @@
         for b in range(spans):
             span = slice(b * lanes, (b + 1) * lanes)
             masked = side_f[b].reshape(half, count, lanes) * pair_mask[:, span][None]
-            out[rows, :, span] = masked.astype(BF16)
-
-    def channels(owner, h):
-        return pl.ds(h * half + owner * part, part)
-
-    def places(h):
-        return pl.ds(h * part, part)
-
-    def left_copy(dest, h):
+            out[span_w, :, :, span] = masked.astype(BF16)
+
+    def channels(owner, ch):
+        return pl.ds(owner * part + edges[ch], edges[ch + 1] - edges[ch])
+
+    def places(ch):
+        return pl.ds(edges[ch], edges[ch + 1] - edges[ch])
+
+    def left_copy(dest, ch, h):
         return remote(
-            left_b.at[channels(dest, h)], left_in.at[slot, places(h)],
-            l_send.at[h], l_recv.at[h], block * per + dest,
-        )
-
-    def right_copy(dest, h):
+            left_b.at[h, channels(dest, ch)], left_in.at[slot, h, places(ch)],
+            l_send.at[ch], l_recv.at[ch], block * per + dest,
+        )
+
+    def right_copy(dest, ch, h):
         return remote(
-            right_b.at[channels(lax.rem(dest, per), h)], right_in.at[me, places(h)],
-            r_send.at[h], r_recv.at[h], dest,
-        )
-
-    def send_block(h):
+            right_b.at[h, channels(lax.rem(dest, per), ch)], right_in.at[me, h, places(ch)],
+            r_send.at[ch], r_recv.at[ch], dest,
+        )
+
+    def send_block(ch, h):
         def one(d):
             owner = lax.rem(slot + 1 + d, per)
-            right_copy(block * per + owner, h).start()
-            left_copy(owner, h).start()
+            right_copy(block * per + owner, ch, h).start()
+            left_copy(owner, ch, h).start()
 
         each(per - 1, one)
 
-    def send_across(h):
+    def send_across(ch, h):
         def one(d):
             near = lax.rem(lax.div(d, plane) + block, 2)
             owner = near * plane + lax.rem(slot + d, plane)
-            right_copy((1 - block) * per + owner, h).start()
+            right_copy((1 - block) * per + owner, ch, h).start()
 
         each(per, one)
 
-    def keep(h):
-        pltpu.make_async_copy(right_b.at[channels(slot, h)], right_in.at[me, places(h)], r_recv.at[h]).start()
-        pltpu.make_async_copy(left_b.at[channels(slot, h)], left_in.at[slot, places(h)], l_recv.at[h]).start()
+    def keep(ch):
+        pltpu.make_async_copy(
+            right_b.at[:, channels(slot, ch)], right_in.at[me, :, places(ch)], r_recv.at[ch]
+        ).start()
+        pltpu.make_async_copy(
+            left_b.at[:, channels(slot, ch)], left_in.at[slot, :, places(ch)], l_recv.at[ch]
+        ).start()
 
     make_side(2, right_b, col)
     pl.semaphore_wait(barrier, groups - 1)
@@ -183,10 +189,14 @@
             if turn == 1:
                 wait_weights(0)
             make_side(2, right_b, h)
-        send_across(h)
+        send_across(0, h)
         make_side(0, left_b, h)
-        send_block(h)
-        keep(h)
+        send_block(0, h)
+    keep(0)
+    every = slice(None)
+    send_across(1, every)
+    send_block(1, every)
+    keep(1)
 
 
     def make_gate(i):
@@ -195,24 +205,27 @@
     each(count, make_gate)
     wait_weights(1)
 
-    def outer_copy(dest, h):
+    def outer_copy(dest, ch):
         return remote(
-            prod.at[dest, places(h)], outer.at[channels(slot, h)],
-            o_send.at[h], o_recv.at[h], block * per + dest,
-        )
-
-    for h in range(cols_n):
-        drain(left_in.at[:, places(h)], l_recv.at[h])
-        drain(right_in.at[:, places(h)], r_recv.at[h])
-        for c in range(h * part, (h + 1) * part):
-            lhs = left_in[:, c].reshape(per * count, length)
-            rhs = right_in[:, c].reshape(length, length)
-            prod[:, c] = dot(lhs, rhs, NT).astype(BF16).reshape(per, count, length)
-        each(per - 1, lambda d: outer_copy(lax.rem(slot + 1 + d, per), h).start())
-        pltpu.make_async_copy(prod.at[slot, places(h)], outer.at[channels(slot, h)], o_recv.at[h]).start()
-
-    for h in range(cols_n):
-        drain(prod.at[:, places(h)], o_recv.at[h])
+            prod.at[dest, :, places(ch)], outer.at[:, channels(slot, ch)],
+            o_send.at[ch], o_recv.at[ch], block * per + dest,
+        )
+
+    for ch in range(chunks):
+        drain(left_in.at[:, :, places(ch)], l_recv.at[ch])
+        drain(right_in.at[:, :, places(ch)], r_recv.at[ch])
+        for h in range(cols_n):
+            for c in range(edges[ch], edges[ch + 1]):
+                lhs = left_in[:, h, c].reshape(per * count, length)
+                rhs = right_in[:, h, c].reshape(length, length)
+                prod[:, h, c] = dot(lhs, rhs, NT).astype(BF16).reshape(per, count, length)
+        each(per - 1, lambda d: outer_copy(lax.rem(slot + 1 + d, per), ch).start())
+        pltpu.make_async_copy(
+            prod.at[slot, :, places(ch)], outer.at[:, channels(slot, ch)], o_recv.at[ch]
+        ).start()
+
+    for ch in range(chunks):
+        drain(prod.at[:, :, places(ch)], o_recv.at[ch])
 
     head_t = head_w[...]
     blank = jnp.zeros((bins, width), BF16)
@@ -225,7 +238,7 @@
     gain_col, shift_col = small[:, 5:6], small[:, 6:7]
     for b in range(spans):
         span = slice(b * lanes, (b + 1) * lanes)
-        values = outer[:, :, span].astype(F32)
+        values = outer[:, :, :, span].astype(F32).reshape(width, count, lanes)
         average = jnp.sum(values, axis=0) * (1.0 / width)
         outer_f[b] = values.reshape(width * count, lanes)
         centred = values - average[None]
@@ -276,10 +289,10 @@
         chosen = jnp.sum(jnp.where(bin_id == targets[i:i + 1, :], symmetric, 0.0), axis=0, keepdims=True)
         loss[i:i + 1, :] = pair_mask[i:i + 1, :] * (total - chosen)
 
-    for h in range(cols_n):
-        drain(left_in.at[pl.ds(0, per - 1), places(h)], l_send.at[h])
-        drain(right_in.at[pl.ds(0, groups - 1), places(h)], r_send.at[h])
-        drain(prod.at[pl.ds(0, per - 1), places(h)], o_send.at[h])
+    for ch in range(chunks):
+        drain(left_in.at[pl.ds(0, per - 1), :, places(ch)], l_send.at[ch])
+        drain(right_in.at[pl.ds(0, groups - 1), :, places(ch)], r_send.at[ch])
+        drain(prod.at[pl.ds(0, per - 1), :, places(ch)], o_send.at[ch])
     drain(logit_in.at[pl.ds(0, groups - 1)], m_send.at[0])
 
 
@@ -300,7 +313,8 @@
     sup = SUPER
     per = groups // sup
     share = width // per
-    chunks = cols_n
+    chunks = 2
+    part, half = share // cols_n, width // cols_n
     packed = 128 // bins
     quads = count // packed
     dma = pltpu.SemaphoreType.DMA
@@ -311,7 +325,7 @@
         head_b.reshape(1, bins),
     )
     update, loss = pl.pallas_call(
-        functools.partial(kernel, rows_n, cols_n, sup),
+        functools.partial(kernel, rows_n, cols_n, sup, chunks),
         out_shape=(
             pltpu.VMEM(pair.shape, BF16),
             pltpu.VMEM((count, length), F32),
@@ -324,12 +338,12 @@
             pltpu.VMEM((width, 8), F32),
             pltpu.VMEM((count, length, width), BF16),
             pltpu.VMEM((length // 128, width // cols_n * count, 128), F32),
-            pltpu.VMEM((width, count, length), BF16),
-            pltpu.VMEM((width, count, length), BF16),
-            pltpu.VMEM((per, share, count, length), BF16),
-            pltpu.VMEM((groups, share, count, length), BF16),
-            pltpu.VMEM((per, share, count, length), BF16),
-            pltpu.VMEM((width, count, length), BF16),
+            pltpu.VMEM((cols_n, half, count, length), BF16),
+            pltpu.VMEM((cols_n, half, count, length), BF16),
+            pltpu.VMEM((per, cols_n, part, count, length), BF16),
+            pltpu.VMEM((groups, cols_n, part, count, length), BF16),
+            pltpu.VMEM((per, cols_n, part, count, length), BF16),
+            pltpu.VMEM((cols_n, half, count, length), BF16),
             pltpu.VMEM((length // 128, width * count, 128), F32),
             pltpu.VMEM((count, length, width), F32),
             pltpu.VMEM((count, length, width), BF16),

time: 30.8 us -> 30.1 us (0.977)
  Pallas kernels: 30.1 us -> 29.3 us
    pallas_call x1, Pallas kernels: 29.3 us -> 28.6 us  [local(): pl.pallas_call(functools.partial(kernel, rows_n, cols_n, sup, chunks), ou...]
where the time goes in v2:
time: 30.1 us; the launch traced here: 30 us
  Pallas kernels  29.3 us (97%)
  between operations  0.64 us (2%)
    pallas_call x1, Pallas kernels, local(): pl.pallas_call(functools.partial(kernel, rows_n, cols_n, sup, chunks), ou...  28.6 us
    pallas_call x1, Pallas kernels, local(): pl.pallas_call(finish, out_shape=(jax.ShapeDtypeStruct(update.shape, upda...  0.72 us

profile of v2, /device:TPU:0, one launch (start us, length us, event | category | flops | bytes accessed | tf_op | source)
XLA Modules:
  0.0 30.0 jit_solution(15634436955539308534)
XLA Ops:
  0.6 28.6 %shard_map.122 = (bf16[8,128,128]{2,1,0:T(8,128)(2,1)S(1)}, f32[8,128]{1,0:T(8,128)S(1)}) custom-call(bf16[8,128,128]{2,1,0:T(8,128)(2,1)} %refs_0_.1, s32[1,128]{1,0:T(1,128)} %bitcast.7, s32[8,128]{1,0:T(8,128)} %refs_2_.1, f32[2,128]{1,0:T(2,128)} %refs_3_.1, f32[2,128]{1,0:T(2,128)} %refs_4_.1, bf16[5,64,128]{2,1,0:T(8,128)(2,1)} %bitcast.5, ...), custom_call_target="tpu_custom_call" | custom-call | tf_op jit(solution)/shard_map/pallas_call | solution.py:327
  29.2 0.7 %shard_map.123 = (bf16[8,128,128]{2,1,0:T(8,128)(2,1)}, f32[8,128]{1,0:T(8,128)}) custom-call(bf16[8,128,128]{2,1,0:T(8,128)(2,1)S(1)} %get-tuple-element.4.update, f32[8,128]{1,0:T(8,128)S(1)} %get-tuple-element.5.loss), custom_call_target="tpu_custom_call" | custom-call | tf_op jit(solution)/shard_map/pallas_call | solution.py:364

commit v3 on v2

--- a/solution.py
+++ b/solution.py
@@ -8,7 +8,8 @@
 from jax.sharding import PartitionSpec as P
 
 SUPER = 2
-CUT = 5
+FEW = 7
+CUT = 6
 F32, BF16 = jnp.float32, jnp.bfloat16
 NT = (((1,), (1,)), ((), ()))
 TN = (((0,), (0,)), ((), ()))
@@ -29,7 +30,7 @@
     wt, wo, small, normed, side_f, right_b, left_b, left_in, right_in, prod, outer, outer_f, gate,
         new_pair, logit_b, logit_in, logit_f, own_t,
         w_send, w_recv, l_send, l_recv, r_send, r_recv, o_send, o_recv, m_send, m_recv,
-        in_sem,
+        in_sem, far_sem,
     ) = rest
     groups = rows_n * cols_n
     count, length, width = pair.shape
@@ -37,8 +38,9 @@
     per = groups // sup
     share = width // per
     part = share // cols_n
-    cut = max(part * CUT // 8, 1)
-    edges = [0, cut, part]
+    few = part * FEW // 8 if part >= 4 else part
+    sizes = (few, 2 * part - few)
+    edges = [[0, max(size * CUT // 8, 1), size] for size in sizes]
     half = w_in.shape[1]
     lanes = 128
     spans = length // lanes
@@ -48,6 +50,9 @@
     me = lax.axis_index("row") * cols_n + col
     block, slot = lax.div(me, per), lax.rem(me, per)
     plane = per // 2
+    layer, place = lax.div(me, plane), lax.rem(me, plane)
+    inner = lax.rem(layer + block, 2) == 1
+    layers = groups // plane
 
     def where(peer):
         return {"row": lax.div(peer, cols_n), "col": lax.rem(peer, cols_n)}
@@ -67,10 +72,14 @@
     barrier = pltpu.get_barrier_semaphore()
 
     def greet(d):
-        pl.semaphore_signal(
-            barrier, inc=1, device_id=where(lax.rem(me + 1 + d, groups)),
-            device_id_type=pl.DeviceIdType.MESH,
-        )
+        peer = lax.rem(me + 1 + d, groups)
+        apart = lax.div(peer, plane) - layer
+
+        @pl.when(apart * apart < 2)
+        def _():
+            pl.semaphore_signal(
+                barrier, inc=1, device_id=where(peer), device_id_type=pl.DeviceIdType.MESH
+            )
 
     each(groups - 1, greet)
 
@@ -136,50 +145,100 @@
             masked = side_f[b].reshape(half, count, lanes) * pair_mask[:, span][None]
             out[span_w, :, :, span] = masked.astype(BF16)
 
-    def channels(owner, ch):
-        return pl.ds(owner * part + edges[ch], edges[ch + 1] - edges[ch])
-
-    def places(ch):
-        return pl.ds(edges[ch], edges[ch + 1] - edges[ch])
-
-    def left_copy(dest, ch, h):
+    def span_of(kind, ch):
+        return edges[kind][ch + 1] - edges[kind][ch]
+
+    def whole(ch):
+        return plane * (span_of(0, ch) + span_of(1, ch))
+
+    def channels(kind, at, ch):
+        return pl.ds(kind * plane * sizes[0] + at * sizes[kind] + edges[kind][ch], span_of(kind, ch))
+
+    def places(kind, ch):
+        return pl.ds(edges[kind][ch], span_of(kind, ch))
+
+    def device(kind, part_of, at):
+        return part_of * per + lax.rem(kind + part_of, 2) * plane + at
+
+    def by_kind(body):
+        pl.when(inner)(functools.partial(body, 1))
+        pl.when(jnp.logical_not(inner))(functools.partial(body, 0))
+
+    def left_copy(kind, at, ch, h):
         return remote(
-            left_b.at[h, channels(dest, ch)], left_in.at[slot, h, places(ch)],
-            l_send.at[ch], l_recv.at[ch], block * per + dest,
+            left_b.at[h, channels(kind, at, ch)], left_in.at[slot, h, places(kind, ch)],
+            l_send.at[ch], l_recv.at[ch], device(kind, block, at),
         )
 
-    def right_copy(dest, ch, h):
+    def right_copy(kind, part_of, at, ch, h, way=0):
         return remote(
-            right_b.at[h, channels(lax.rem(dest, per), ch)], right_in.at[me, h, places(ch)],
-            r_send.at[ch], r_recv.at[ch], dest,
+            right_b.at[h, channels(kind, at, ch)], right_in.at[me, h, places(kind, ch)],
+            r_send.at[ch], r_recv.at[way, ch], device(kind, part_of, at),
         )
 
+    def pass_on(ch):
+        def one(d):
+            piece = right_in.at[3 * block * plane + lax.rem(place + d, plane), :, places(1, ch)]
+            remote(
+                piece, piece, r_send.at[ch], r_recv.at[0, ch], device(1, 1 - block, place)
+            ).start()
+
+        each(plane, one)
+
+    def send_right(kind, ch, h):
+        way = kind * (1 - inner.astype(jnp.int32))
+
+        def one(d):
+            at = lax.rem(place + d, plane)
+
+            @pl.when(device(kind, block, at) != me)
+            def _():
+                right_copy(kind, block, at, ch, h, way).start()
+
+        each(plane, one)
+
+    def send_left(kind, ch, h):
+        def one(d):
+            at = lax.rem(place + d, plane)
+
+            @pl.when(device(kind, block, at) != me)
+            def _():
+                left_copy(kind, at, ch, h).start()
+
+        each(plane, one)
+
     def send_block(ch, h):
+        for kind in (1, 0):
+            send_right(kind, ch, h)
+            send_left(kind, ch, h)
+
+    def send_across(kind, ch, h):
         def one(d):
-            owner = lax.rem(slot + 1 + d, per)
-            right_copy(block * per + owner, ch, h).start()
-            left_copy(owner, ch, h).start()
-
-        each(per - 1, one)
-
-    def send_across(ch, h):
-        def one(d):
-            near = lax.rem(lax.div(d, plane) + block, 2)
-            owner = near * plane + lax.rem(slot + d, plane)
-            right_copy((1 - block) * per + owner, ch, h).start()
-
-        each(per, one)
+            right_copy(kind, 1 - block, lax.rem(place + d, plane), ch, h).start()
+
+        each(plane, one)
 
     def keep(ch):
-        pltpu.make_async_copy(
-            right_b.at[:, channels(slot, ch)], right_in.at[me, :, places(ch)], r_recv.at[ch]
-        ).start()
-        pltpu.make_async_copy(
-            left_b.at[:, channels(slot, ch)], left_in.at[slot, :, places(ch)], l_recv.at[ch]
-        ).start()
+        def own(kind):
+            pltpu.make_async_copy(
+                right_b.at[:, channels(kind, place, ch)], right_in.at[me, :, places(kind, ch)], r_recv.at[0, ch]
+            ).start()
+            pltpu.make_async_copy(
+                left_b.at[:, channels(kind, place, ch)], left_in.at[slot, :, places(kind, ch)], l_recv.at[ch]
+            ).start()
+
+        by_kind(own)
 
     make_side(2, right_b, col)
-    pl.semaphore_wait(barrier, groups - 1)
+    pl.semaphore_wait(barrier, plane * (2 + inner.astype(jnp.int32)) - 1)
+
+    def tell(peer):
+        pl.semaphore_signal(far_sem, inc=1, device_id=where(peer), device_id_type=pl.DeviceIdType.MESH)
+
+    @pl.when(inner)
+    def _():
+        tell(me + plane - 2 * plane * block)
+
     for d in range(1, cols_n):
         for copy in weight_copies(lax.rem(col + d, cols_n)):
             copy.start()
@@ -189,43 +248,79 @@
             if turn == 1:
                 wait_weights(0)
             make_side(2, right_b, h)
-        send_across(0, h)
+        pl.when(inner)(functools.partial(send_across, 1, 0, h))
+        pl.when(jnp.logical_not(inner))(functools.partial(send_right, 1, 0, h))
         make_side(0, left_b, h)
-        send_block(0, h)
+        send_left(1, 0, h)
+        pl.when(inner)(functools.partial(send_right, 1, 0, h))
+        send_left(0, 0, h)
+        send_right(0, 0, h)
     keep(0)
     every = slice(None)
-    send_across(1, every)
-    send_block(1, every)
+
+    @pl.when(jnp.logical_not(inner))
+    def _():
+        send_right(1, 1, every)
+
+    pl.semaphore_wait(far_sem, 1)
+
+    @pl.when(inner)
+    def _():
+        tell(me - plane + 2 * plane * block)
+        send_across(0, 0, every)
+        send_across(0, 1, every)
+        send_block(1, every)
+
+    @pl.when(jnp.logical_not(inner))
+    def _():
+        send_across(0, 0, every)
+        send_left(1, 1, every)
+        send_left(0, 1, every)
+        send_right(0, 1, every)
+        send_across(0, 1, every)
+
     keep(1)
-
 
     def make_gate(i):
         gate[i] = jax.nn.sigmoid(dot(normed[i], wt[4], NT) + b_in[4:5, :])
 
     each(count, make_gate)
+
+    @pl.when(inner)
+    def _():
+        for ch in range(chunks):
+            drain(right_in.at[pl.ds(0, plane), :, places(1, ch)], r_recv.at[1, ch])
+            pass_on(ch)
+            if ch == 0:
+                send_across(1, 1, every)
+
     wait_weights(1)
 
-    def outer_copy(dest, ch):
-        return remote(
-            prod.at[dest, :, places(ch)], outer.at[:, channels(slot, ch)],
-            o_send.at[ch], o_recv.at[ch], block * per + dest,
-        )
+    def multiply(kind):
+        def outer_copy(dest, ch):
+            return remote(
+                prod.at[dest, :, places(kind, ch)], outer.at[:, channels(kind, place, ch)],
+                o_send.at[ch], o_recv.at[ch], block * per + dest,
+            )
+
+        for ch in range(chunks):
+            now = places(kind, ch)
+            drain(left_in.at[:, :, now], l_recv.at[ch])
+            drain(right_in.at[pl.ds(0, groups - kind * plane), :, now], r_recv.at[0, ch])
+            for h in range(cols_n):
+                for c in range(edges[kind][ch], edges[kind][ch + 1]):
+                    lhs = left_in[:, h, c].reshape(per * count, length)
+                    rhs = right_in[:, h, c].reshape(length, length)
+                    prod[:, h, c] = dot(lhs, rhs, NT).astype(BF16).reshape(per, count, length)
+            each(per - 1, lambda d: outer_copy(lax.rem(slot + 1 + d, per), ch).start())
+            pltpu.make_async_copy(
+                prod.at[slot, :, now], outer.at[:, channels(kind, place, ch)], o_recv.at[ch]
+            ).start()
+
+    by_kind(multiply)
 
     for ch in range(chunks):
-        drain(left_in.at[:, :, places(ch)], l_recv.at[ch])
-        drain(right_in.at[:, :, places(ch)], r_recv.at[ch])
-        for h in range(cols_n):
-            for c in range(edges[ch], edges[ch + 1]):
-                lhs = left_in[:, h, c].reshape(per * count, length)
-                rhs = right_in[:, h, c].reshape(length, length)
-                prod[:, h, c] = dot(lhs, rhs, NT).astype(BF16).reshape(per, count, length)
-        each(per - 1, lambda d: outer_copy(lax.rem(slot + 1 + d, per), ch).start())
-        pltpu.make_async_copy(
-            prod.at[slot, :, places(ch)], outer.at[:, channels(slot, ch)], o_recv.at[ch]
-        ).start()
-
-    for ch in range(chunks):
-        drain(prod.at[:, :, places(ch)], o_recv.at[ch])
+        drain(outer.at[:, pl.ds(0, whole(ch))], o_recv.at[ch])
 
     head_t = head_w[...]
     blank = jnp.zeros((bins, width), BF16)
@@ -277,6 +372,18 @@
     order = ((at % fold) // quads) * count + (at // fold) * quads + at % quads
     shuffle = jnp.where(order == to, 1.0, 0.0).astype(BF16)
 
+    def sent(kind):
+        for ch in range(chunks):
+            drain(left_b.at[:, pl.ds(0, whole(ch) - span_of(kind, ch))], l_send.at[ch])
+            drain(right_b.at[:, pl.ds(0, whole(ch) - span_of(kind, ch))], r_send.at[ch])
+            drain(right_b.at[:, pl.ds(0, plane * span_of(0, ch))], r_send.at[ch])
+            if kind:
+                for _ in range(2):
+                    drain(right_b.at[:, pl.ds(0, plane * span_of(1, ch))], r_send.at[ch])
+            drain(prod.at[pl.ds(0, per - 1), :, places(kind, ch)], o_send.at[ch])
+
+    by_kind(sent)
+
     drain(logit_in, m_recv.at[0])
     logit_f[...] = logit_in[...].astype(F32).reshape(logit_f.shape)
     bin_id = lax.broadcasted_iota(jnp.int32, (bins, length), 0)
@@ -289,10 +396,6 @@
         chosen = jnp.sum(jnp.where(bin_id == targets[i:i + 1, :], symmetric, 0.0), axis=0, keepdims=True)
         loss[i:i + 1, :] = pair_mask[i:i + 1, :] * (total - chosen)
 
-    for ch in range(chunks):
-        drain(left_in.at[pl.ds(0, per - 1), :, places(ch)], l_send.at[ch])
-        drain(right_in.at[pl.ds(0, groups - 1), :, places(ch)], r_send.at[ch])
-        drain(prod.at[pl.ds(0, per - 1), :, places(ch)], o_send.at[ch])
     drain(logit_in.at[pl.ds(0, groups - 1)], m_send.at[0])
 
 
@@ -315,6 +418,7 @@
     share = width // per
     chunks = 2
     part, half = share // cols_n, width // cols_n
+    most = 2 * part - (part * FEW // 8 if part >= 4 else part)
     packed = 128 // bins
     quads = count // packed
     dma = pltpu.SemaphoreType.DMA
@@ -340,9 +444,9 @@
             pltpu.VMEM((length // 128, width // cols_n * count, 128), F32),
             pltpu.VMEM((cols_n, half, count, length), BF16),
             pltpu.VMEM((cols_n, half, count, length), BF16),
-            pltpu.VMEM((per, cols_n, part, count, length), BF16),
-            pltpu.VMEM((groups, cols_n, part, count, length), BF16),
-            pltpu.VMEM((per, cols_n, part, count, length), BF16),
+            pltpu.VMEM((per, cols_n, most, count, length), BF16),
+            pltpu.VMEM((groups, cols_n, most, count, length), BF16),
+            pltpu.VMEM((per, cols_n, most, count, length), BF16),
             pltpu.VMEM((cols_n, half, count, length), BF16),
             pltpu.VMEM((length // 128, width * count, 128), F32),
             pltpu.VMEM((count, length, width), F32),
@@ -352,9 +456,9 @@
             pltpu.VMEM((groups * quads * count, 128), F32),
             pltpu.VMEM((count, bins, length), F32),
             dma((2, cols_n)), dma((2, cols_n)),
-            dma((chunks,)), dma((chunks,)), dma((chunks,)), dma((chunks,)), dma((chunks,)), dma((chunks,)),
+            dma((chunks,)), dma((chunks,)), dma((chunks,)), dma((2, chunks)), dma((chunks,)), dma((chunks,)),
             dma((1,)), dma((1,)),
-            dma((11,)),
+            dma((11,)), pltpu.SemaphoreType.REGULAR,
         ],
         compiler_params=pltpu.CompilerParams(
             collective_id=0, has_side_effects=True, vmem_limit_bytes=60 * 1024 * 1024

time: 30.1 us -> 29.5 us (0.980)
  Pallas kernels: 29.3 us -> 28.7 us
    pallas_call x1, Pallas kernels: 28.6 us -> 28 us  [local(): pl.pallas_call(functools.partial(kernel, rows_n, cols_n, sup, chunks), ou...]
where the time goes in v3:
time: 29.5 us; the launch traced here: 29.3 us
  Pallas kernels  28.7 us (97%)
  between operations  0.64 us (2%)
    pallas_call x1, Pallas kernels, local(): pl.pallas_call(functools.partial(kernel, rows_n, cols_n, sup, chunks), ou...  28 us
    pallas_call x1, Pallas kernels, local(): pl.pallas_call(finish, out_shape=(jax.ShapeDtypeStruct(update.shape, upda...  0.72 us

profile of v3, /device:TPU:0, one launch (start us, length us, event | category | flops | bytes accessed | tf_op | source)
XLA Modules:
  0.0 29.3 jit_solution(10962243073171308764)
XLA Ops:
  0.6 28.0 %shard_map.122 = (bf16[8,128,128]{2,1,0:T(8,128)(2,1)S(1)}, f32[8,128]{1,0:T(8,128)S(1)}) custom-call(bf16[8,128,128]{2,1,0:T(8,128)(2,1)} %refs_0_.1, s32[1,128]{1,0:T(1,128)} %bitcast.7, s32[8,128]{1,0:T(8,128)} %refs_2_.1, f32[2,128]{1,0:T(2,128)} %refs_3_.1, f32[2,128]{1,0:T(2,128)} %refs_4_.1, bf16[5,64,128]{2,1,0:T(8,128)(2,1)} %bitcast.5, ...), custom_call_target="tpu_custom_call" | custom-call | tf_op jit(solution)/shard_map/pallas_call | solution.py:431
  28.6 0.7 %shard_map.123 = (bf16[8,128,128]{2,1,0:T(8,128)(2,1)}, f32[8,128]{1,0:T(8,128)}) custom-call(bf16[8,128,128]{2,1,0:T(8,128)(2,1)S(1)} %get-tuple-element.4.update, f32[8,128]{1,0:T(8,128)S(1)} %get-tuple-element.5.loss), custom_call_target="tpu_custom_call" | custom-call | tf_op jit(solution)/shard_map/pallas_call | solution.py:468

commit v4 on v3

--- a/solution.py
+++ b/solution.py
@@ -30,7 +30,7 @@
     wt, wo, small, normed, side_f, right_b, left_b, left_in, right_in, prod, outer, outer_f, gate,
         new_pair, logit_b, logit_in, logit_f, own_t,
         w_send, w_recv, l_send, l_recv, r_send, r_recv, o_send, o_recv, m_send, m_recv,
-        in_sem, far_sem,
+        in_sem, far_sem, spread_w, shuffle,
     ) = rest
     groups = rows_n * cols_n
     count, length, width = pair.shape
@@ -296,6 +296,18 @@
 
     wait_weights(1)
 
+    head_t = head_w[...]
+    spread_w[...] = jnp.zeros(spread_w.shape, BF16)
+    for p in range(packed):
+        spread_w[p, p * bins:(p + 1) * bins, :] = head_t
+    bias_row = jnp.concatenate([head_b[...]] * packed, axis=1)
+
+    at = lax.broadcasted_iota(jnp.int32, (length, length), 0)
+    to = lax.broadcasted_iota(jnp.int32, (length, length), 1)
+    fold = length // packed
+    order = ((at % fold) // quads) * count + (at // fold) * quads + at % quads
+    shuffle[...] = jnp.where(order == to, 1.0, 0.0).astype(BF16)
+
     def multiply(kind):
         def outer_copy(dest, ch):
             return remote(
@@ -319,25 +331,46 @@
 
     by_kind(multiply)
 
+    def pieces(ch):
+        for kind in range(2):
+            for at in range(plane):
+                start = kind * plane * sizes[0] + at * sizes[kind] + edges[kind][ch]
+                yield start, start + span_of(kind, ch)
+
+    stats = [None] * spans
     for ch in range(chunks):
         drain(outer.at[:, pl.ds(0, whole(ch))], o_recv.at[ch])
-
-    head_t = head_w[...]
-    blank = jnp.zeros((bins, width), BF16)
-    spread_w = [
-        jnp.concatenate([head_t if h == p else blank for h in range(packed)], axis=0)
-        for p in range(packed)
-    ]
-    bias_row = jnp.concatenate([head_b[...]] * packed, axis=1)
+        if not whole(ch):
+            continue
+        for b in range(spans):
+            amount = cols_n * whole(ch)
+            span = slice(b * lanes, (b + 1) * lanes)
+            loaded, added = [], 0.0
+            for h in range(cols_n):
+                for start, stop in pieces(ch):
+                    values = outer[h, start:stop, :, span].astype(F32)
+                    rows = slice((h * half + start) * count, (h * half + stop) * count)
+                    outer_f[b, rows, :] = values.reshape((stop - start) * count, lanes)
+                    added = added + jnp.sum(values, axis=0)
+                    loaded.append((h, start, stop))
+            middle, scatter = added * (1.0 / amount), 0.0
+            for h, start, stop in loaded:
+                rows = slice((h * half + start) * count, (h * half + stop) * count)
+                centred = outer_f[b, rows, :].reshape(stop - start, count, lanes) - middle[None]
+                scatter = scatter + jnp.sum(centred * centred, axis=0)
+            if stats[b] is not None:
+                before, mean_b, scatter_b = stats[b]
+                apart = middle - mean_b
+                scatter = scatter_b + scatter + apart * apart * (before * amount / (before + amount))
+                middle = mean_b + apart * (amount / (before + amount))
+                amount = before + amount
+            stats[b] = (amount, middle, scatter)
 
     gain_col, shift_col = small[:, 5:6], small[:, 6:7]
     for b in range(spans):
         span = slice(b * lanes, (b + 1) * lanes)
-        values = outer[:, :, :, span].astype(F32).reshape(width, count, lanes)
-        average = jnp.sum(values, axis=0) * (1.0 / width)
-        outer_f[b] = values.reshape(width * count, lanes)
-        centred = values - average[None]
-        inverse = lax.rsqrt(jnp.sum(centred * centred, axis=0) * (1.0 / width) + 1.0)
+        average = stats[b][1]
+        inverse = lax.rsqrt(stats[b][2] * (1.0 / width) + 1.0)
         for i in range(count):
             part_i = outer_f[b, pl.ds(i, width, stride=count), :]
             part_i = (part_i - average[i:i + 1, :]) * inverse[i:i + 1, :] * gain_col + shift_col
@@ -354,11 +387,11 @@
     def logit_copy(dest):
         return remote(
             logit_b.at[dest], logit_in.at[me],
-            m_send.at[0], m_recv.at[0], dest,
+            m_send.at[0], m_recv.at[layer], dest,
         )
 
     logit_local = pltpu.make_async_copy(
-        logit_b.at[me], logit_in.at[me], m_recv.at[0]
+        logit_b.at[me], logit_in.at[me], m_recv.at[layer]
     )
     each(groups - 1, lambda d: logit_copy(lax.rem(me + 1 + d, groups)).start())
     logit_local.start()
@@ -366,12 +399,6 @@
     bias_col = jnp.concatenate([head_b[...], jnp.zeros((7, bins), F32)], axis=0).T[:, 0:1]
     for i in range(count):
         own_t[i] = dot(head_t, new_pair[i], NT) + bias_col
-    at = lax.broadcasted_iota(jnp.int32, (length, length), 0)
-    to = lax.broadcasted_iota(jnp.int32, (length, length), 1)
-    fold = length // packed
-    order = ((at % fold) // quads) * count + (at // fold) * quads + at % quads
-    shuffle = jnp.where(order == to, 1.0, 0.0).astype(BF16)
-
     def sent(kind):
         for ch in range(chunks):
             drain(left_b.at[:, pl.ds(0, whole(ch) - span_of(kind, ch))], l_send.at[ch])
@@ -384,13 +411,17 @@
 
     by_kind(sent)
 
-    drain(logit_in, m_recv.at[0])
-    logit_f[...] = logit_in[...].astype(F32).reshape(logit_f.shape)
+    tall = plane * quads * count
+    for d in range(layers):
+        at = lax.rem(layer + d, layers)
+        some = logit_in.at[pl.ds(at * plane, plane)]
+        drain(some, m_recv.at[at])
+        logit_f[pl.ds(pl.multiple_of(at * tall, tall), tall), :] = some[...].astype(F32).reshape(tall, packed * bins)
     bin_id = lax.broadcasted_iota(jnp.int32, (bins, length), 0)
     for i in range(count):
         flipped = logit_f[pl.ds(i, groups * quads, stride=count), :].T
         flipped = jnp.concatenate([flipped[p * bins:(p + 1) * bins] for p in range(packed)], axis=1)
-        symmetric = own_t[i] + dot(flipped.astype(BF16), shuffle)
+        symmetric = own_t[i] + dot(flipped.astype(BF16), shuffle[...])
         top = jnp.max(symmetric, axis=0, keepdims=True)
         total = top + jnp.log(jnp.sum(jnp.exp(symmetric - top), axis=0, keepdims=True))
         chosen = jnp.sum(jnp.where(bin_id == targets[i:i + 1, :], symmetric, 0.0), axis=0, keepdims=True)
@@ -457,8 +488,9 @@
             pltpu.VMEM((count, bins, length), F32),
             dma((2, cols_n)), dma((2, cols_n)),
             dma((chunks,)), dma((chunks,)), dma((chunks,)), dma((2, chunks)), dma((chunks,)), dma((chunks,)),
-            dma((1,)), dma((1,)),
+            dma((1,)), dma((groups // (per // 2),)),
             dma((11,)), pltpu.SemaphoreType.REGULAR,
+            pltpu.VMEM((packed, 128, width), BF16), pltpu.VMEM((length, length), BF16),
         ],
         compiler_params=pltpu.CompilerParams(
             collective_id=0, has_side_effects=True, vmem_limit_bytes=60 * 1024 * 1024

time: 29.5 us -> 29.3 us (level)
  no operation moved by 1% of the time
where the time goes in v4:
time: 29.3 us; the launch traced here: 29.1 us
  Pallas kernels  28.5 us (97%)
  between operations  0.64 us (2%)
    pallas_call x1, Pallas kernels, local(): pl.pallas_call(functools.partial(kernel, rows_n, cols_n, sup, chunks), ou...  27.8 us
    pallas_call x1, Pallas kernels, local(): pl.pallas_call(finish, out_shape=(jax.ShapeDtypeStruct(update.shape, upda...  0.72 us

profile of v4, /device:TPU:0, one launch (start us, length us, event | category | flops | bytes accessed | tf_op | source)
XLA Modules:
  0.0 29.1 jit_solution(13048418325859252808)
XLA Ops:
  0.6 27.8 %shard_map.122 = (bf16[8,128,128]{2,1,0:T(8,128)(2,1)S(1)}, f32[8,128]{1,0:T(8,128)S(1)}) custom-call(bf16[8,128,128]{2,1,0:T(8,128)(2,1)} %refs_0_.1, s32[1,128]{1,0:T(1,128)} %bitcast.7, s32[8,128]{1,0:T(8,128)} %refs_2_.1, f32[2,128]{1,0:T(2,128)} %refs_3_.1, f32[2,128]{1,0:T(2,128)} %refs_4_.1, bf16[5,64,128]{2,1,0:T(8,128)(2,1)} %bitcast.5, ...), custom_call_target="tpu_custom_call" | custom-call | tf_op jit(solution)/shard_map/pallas_call | solution.py:462
  28.4 0.7 %shard_map.123 = (bf16[8,128,128]{2,1,0:T(8,128)(2,1)}, f32[8,128]{1,0:T(8,128)}) custom-call(bf16[8,128,128]{2,1,0:T(8,128)(2,1)S(1)} %get-tuple-element.4.update, f32[8,128]{1,0:T(8,128)S(1)} %get-tuple-element.5.loss), custom_call_target="tpu_custom_call" | custom-call | tf_op jit(solution)/shard_map/pallas_call | solution.py:500

commit v5 on v4

--- a/solution.py
+++ b/solution.py
@@ -29,7 +29,7 @@
     (
     wt, wo, small, normed, side_f, right_b, left_b, left_in, right_in, prod, outer, outer_f, gate,
         new_pair, logit_b, logit_in, logit_f, own_t,
-        w_send, w_recv, l_send, l_recv, r_send, r_recv, o_send, o_recv, m_send, m_recv,
+        sent_sem, w_recv, l_recv, r_recv, o_recv, m_recv,
         in_sem, far_sem, spread_w, shuffle,
     ) = rest
     groups = rows_n * cols_n
@@ -66,7 +66,7 @@
     def each(n, body):
         lax.fori_loop(0, n, lambda i, c: (body(i), c)[1], 0, unroll=True)
 
-    loads = [pltpu.make_async_copy(sources[n], held[n], in_sem.at[n]) for n in range(11)]
+    loads = [pltpu.make_async_copy(sources[n], held[n], in_sem.at[0]) for n in range(11)]
     for load in loads:
         load.start()
     barrier = pltpu.get_barrier_semaphore()
@@ -115,8 +115,8 @@
     def weight_copies(peer_col):
         peer = me - col + peer_col
         return (
-            remote(wt.at[:, mine, :], wt.at[:, mine, :], w_send.at[0, peer_col], w_recv.at[0, col], peer),
-            remote(wo.at[mine, :], wo.at[mine, :], w_send.at[1, peer_col], w_recv.at[1, col], peer),
+            remote(wt.at[:, mine, :], wt.at[:, mine, :], sent_sem.at[0], w_recv.at[0], peer),
+            remote(wo.at[mine, :], wo.at[mine, :], sent_sem.at[0], w_recv.at[1], peer),
         )
 
     def wait_weights(which):
@@ -124,10 +124,7 @@
             peer_col = lax.rem(col + d, cols_n)
             theirs = pl.ds(pl.multiple_of(peer_col * half, half), half)
             ref = (wt.at[:, theirs, :], wo.at[theirs, :])[which]
-            mine_ref = (wt.at[:, mine, :], wo.at[mine, :])[which]
-            peer = me - col + peer_col
-            remote(ref, ref, w_send.at[which, peer_col], w_recv.at[which, peer_col], peer).wait_recv()
-            remote(mine_ref, mine_ref, w_send.at[which, peer_col], w_recv.at[which, peer_col], peer).wait_send()
+            drain(ref, w_recv.at[which])
 
     def make_side(first, out, span_w):
         start = pl.multiple_of(span_w * half, half)
@@ -167,20 +164,20 @@
     def left_copy(kind, at, ch, h):
         return remote(
             left_b.at[h, channels(kind, at, ch)], left_in.at[slot, h, places(kind, ch)],
-            l_send.at[ch], l_recv.at[ch], device(kind, block, at),
+            sent_sem.at[0], l_recv.at[ch], device(kind, block, at),
         )
 
     def right_copy(kind, part_of, at, ch, h, way=0):
         return remote(
             right_b.at[h, channels(kind, at, ch)], right_in.at[me, h, places(kind, ch)],
-            r_send.at[ch], r_recv.at[way, ch], device(kind, part_of, at),
+            sent_sem.at[0], r_recv.at[way, ch], device(kind, part_of, at),
         )
 
     def pass_on(ch):
         def one(d):
             piece = right_in.at[3 * block * plane + lax.rem(place + d, plane), :, places(1, ch)]
             remote(
-                piece, piece, r_send.at[ch], r_recv.at[0, ch], device(1, 1 - block, place)
+                piece, piece, sent_sem.at[0], r_recv.at[0, ch], device(1, 1 - block, place)
             ).start()
 
         each(plane, one)
@@ -312,7 +309,7 @@
         def outer_copy(dest, ch):
             return remote(
                 prod.at[dest, :, places(kind, ch)], outer.at[:, channels(kind, place, ch)],
-                o_send.at[ch], o_recv.at[ch], block * per + dest,
+                sent_sem.at[0], o_recv.at[ch], block * per + dest,
             )
 
         for ch in range(chunks):
@@ -387,7 +384,7 @@
     def logit_copy(dest):
         return remote(
             logit_b.at[dest], logit_in.at[me],
-            m_send.at[0], m_recv.at[layer], dest,
+            sent_sem.at[0], m_recv.at[layer], dest,
         )
 
     logit_local = pltpu.make_async_copy(
@@ -400,14 +397,17 @@
     for i in range(count):
         own_t[i] = dot(head_t, new_pair[i], NT) + bias_col
     def sent(kind):
+        for _ in range(1, cols_n):
+            drain(wt.at[:, mine, :], sent_sem.at[0])
+            drain(wo.at[mine, :], sent_sem.at[0])
         for ch in range(chunks):
-            drain(left_b.at[:, pl.ds(0, whole(ch) - span_of(kind, ch))], l_send.at[ch])
-            drain(right_b.at[:, pl.ds(0, whole(ch) - span_of(kind, ch))], r_send.at[ch])
-            drain(right_b.at[:, pl.ds(0, plane * span_of(0, ch))], r_send.at[ch])
+            drain(left_b.at[:, pl.ds(0, whole(ch) - span_of(kind, ch))], sent_sem.at[0])
+            drain(right_b.at[:, pl.ds(0, whole(ch) - span_of(kind, ch))], sent_sem.at[0])
+            drain(right_b.at[:, pl.ds(0, plane * span_of(0, ch))], sent_sem.at[0])
             if kind:
                 for _ in range(2):
-                    drain(right_b.at[:, pl.ds(0, plane * span_of(1, ch))], r_send.at[ch])
-            drain(prod.at[pl.ds(0, per - 1), :, places(kind, ch)], o_send.at[ch])
+                    drain(right_b.at[:, pl.ds(0, plane * span_of(1, ch))], sent_sem.at[0])
+            drain(prod.at[pl.ds(0, per - 1), :, places(kind, ch)], sent_sem.at[0])
 
     by_kind(sent)
 
@@ -427,7 +427,7 @@
         chosen = jnp.sum(jnp.where(bin_id == targets[i:i + 1, :], symmetric, 0.0), axis=0, keepdims=True)
         loss[i:i + 1, :] = pair_mask[i:i + 1, :] * (total - chosen)
 
-    drain(logit_in.at[pl.ds(0, groups - 1)], m_send.at[0])
+    drain(logit_in.at[pl.ds(0, groups - 1)], sent_sem.at[0])
 
 
 def finish(update, loss, update_out, loss_out, sem):
@@ -486,10 +486,9 @@
             pltpu.VMEM((groups, quads, count, 128), BF16),
             pltpu.VMEM((groups * quads * count, 128), F32),
             pltpu.VMEM((count, bins, length), F32),
-            dma((2, cols_n)), dma((2, cols_n)),
-            dma((chunks,)), dma((chunks,)), dma((chunks,)), dma((2, chunks)), dma((chunks,)), dma((chunks,)),
-            dma((1,)), dma((groups // (per // 2),)),
-            dma((11,)), pltpu.SemaphoreType.REGULAR,
+            dma((1,)), dma((2,)), dma((chunks,)), dma((2, chunks)), dma((chunks,)),
+            dma((groups // (per // 2),)),
+            dma((1,)), pltpu.SemaphoreType.REGULAR,
             pltpu.VMEM((packed, 128, width), BF16), pltpu.VMEM((length, length), BF16),
         ],
         compiler_params=pltpu.CompilerParams(

time: 29.3 us -> 29.1 us (level)
  no operation moved by 1% of the time
where the time goes in v5:
time: 29.1 us; the launch traced here: 28.9 us
  Pallas kernels  28.3 us (97%)
  between operations  0.64 us (2%)
    pallas_call x1, Pallas kernels, local(): pl.pallas_call(functools.partial(kernel, rows_n, cols_n, sup, chunks), ou...  27.6 us
    pallas_call x1, Pallas kernels, local(): pl.pallas_call(finish, out_shape=(jax.ShapeDtypeStruct(update.shape, upda...  0.72 us

profile of v5, /device:TPU:0, one launch (start us, length us, event | category | flops | bytes accessed | tf_op | source)
XLA Modules:
  0.0 28.9 jit_solution(7310681377302118393)
XLA Ops:
  0.6 27.6 %shard_map.122 = (bf16[8,128,128]{2,1,0:T(8,128)(2,1)S(1)}, f32[8,128]{1,0:T(8,128)S(1)}) custom-call(bf16[8,128,128]{2,1,0:T(8,128)(2,1)} %refs_0_.1, s32[1,128]{1,0:T(1,128)} %bitcast.7, s32[8,128]{1,0:T(8,128)} %refs_2_.1, f32[2,128]{1,0:T(2,128)} %refs_3_.1, f32[2,128]{1,0:T(2,128)} %refs_4_.1, bf16[5,64,128]{2,1,0:T(8,128)(2,1)} %bitcast.5, ...), custom_call_target="tpu_custom_call" | custom-call | tf_op jit(solution)/shard_map/pallas_call | solution.py:462
  28.2 0.7 %shard_map.123 = (bf16[8,128,128]{2,1,0:T(8,128)(2,1)}, f32[8,128]{1,0:T(8,128)}) custom-call(bf16[8,128,128]{2,1,0:T(8,128)(2,1)S(1)} %get-tuple-element.4.update, f32[8,128]{1,0:T(8,128)S(1)} %get-tuple-element.5.loss), custom_call_target="tpu_custom_call" | custom-call | tf_op jit(solution)/shard_map/pallas_call | solution.py:499

commit v6 on v5

--- a/solution.py
+++ b/solution.py
@@ -66,7 +66,7 @@
     def each(n, body):
         lax.fori_loop(0, n, lambda i, c: (body(i), c)[1], 0, unroll=True)
 
-    loads = [pltpu.make_async_copy(sources[n], held[n], in_sem.at[0]) for n in range(11)]
+    loads = [pltpu.make_async_copy(sources[n], held[n], in_sem.at[int(n not in (0, 3, 4))]) for n in range(11)]
     for load in loads:
         load.start()
     barrier = pltpu.get_barrier_semaphore()
@@ -87,11 +87,9 @@
         pltpu.make_async_copy(ref, ref, sem).wait()
 
 
-    for load in loads:
-        load.wait()
+    for n in (0, 3, 4):
+        loads[n].wait()
     mine = pl.ds(pl.multiple_of(col * half, half), half)
-    wt[:, mine, :] = w_in[...]
-    wo[mine, :] = w_out[...]
 
     def norm_rows(i):
         values = pair[i].astype(F32)
@@ -101,6 +99,10 @@
         normed[i] = scaled.astype(BF16)
 
     each(count, norm_rows)
+    for n in (1, 2, 5, 6, 7, 8, 9, 10):
+        loads[n].wait()
+    wt[:, mine, :] = w_in[...]
+    wo[mine, :] = w_out[...]
 
     row_mask = mask[...].astype(F32)
     lane = lax.broadcasted_iota(jnp.int32, (count, length), 1)
@@ -488,7 +490,7 @@
             pltpu.VMEM((count, bins, length), F32),
             dma((1,)), dma((2,)), dma((chunks,)), dma((2, chunks)), dma((chunks,)),
             dma((groups // (per // 2),)),
-            dma((1,)), pltpu.SemaphoreType.REGULAR,
+            dma((2,)), pltpu.SemaphoreType.REGULAR,
             pltpu.VMEM((packed, 128, width), BF16), pltpu.VMEM((length, length), BF16),
         ],
         compiler_params=pltpu.CompilerParams(

time: 29.1 us -> 29.1 us (level)
  no operation moved by 1% of the time
where the time goes in v6:
time: 29.1 us; the launch traced here: 29 us
  Pallas kernels  28.3 us (97%)
  between operations  0.64 us (2%)
    pallas_call x1, Pallas kernels, local(): pl.pallas_call(functools.partial(kernel, rows_n, cols_n, sup, chunks), ou...  27.6 us
    pallas_call x1, Pallas kernels, local(): pl.pallas_call(finish, out_shape=(jax.ShapeDtypeStruct(update.shape, upda...  0.72 us

profile of v6, /device:TPU:0, one launch (start us, length us, event | category | flops | bytes accessed | tf_op | source)
XLA Modules:
  0.0 29.0 jit_solution(10805256119699938201)
XLA Ops:
  0.6 27.6 %shard_map.122 = (bf16[8,128,128]{2,1,0:T(8,128)(2,1)S(1)}, f32[8,128]{1,0:T(8,128)S(1)}) custom-call(bf16[8,128,128]{2,1,0:T(8,128)(2,1)} %refs_0_.1, s32[1,128]{1,0:T(1,128)} %bitcast.7, s32[8,128]{1,0:T(8,128)} %refs_2_.1, f32[2,128]{1,0:T(2,128)} %refs_3_.1, f32[2,128]{1,0:T(2,128)} %refs_4_.1, bf16[5,64,128]{2,1,0:T(8,128)(2,1)} %bitcast.5, ...), custom_call_target="tpu_custom_call" | custom-call | tf_op jit(solution)/shard_map/pallas_call | solution.py:464
  28.2 0.7 %shard_map.123 = (bf16[8,128,128]{2,1,0:T(8,128)(2,1)}, f32[8,128]{1,0:T(8,128)}) custom-call(bf16[8,128,128]{2,1,0:T(8,128)(2,1)S(1)} %get-tuple-element.4.update, f32[8,128]{1,0:T(8,128)S(1)} %get-tuple-element.5.loss), custom_call_target="tpu_custom_call" | custom-call | tf_op jit(solution)/shard_map/pallas_call | solution.py:501
